TPU v7x, 32 devices: a whole 2x2x4 slice. The times are simulated.
32 devices in a mesh: row: 4 (over z), col: 2 (over x), dp: 4 (over y, core).
Axes of the slice: x: 2, y: 2, z: 4, core: 2. Of those that a mesh axis runs over, the one named last changes fastest.
Arguments:
- tokens: bfloat16 [1536, 6144], P('dp', 'row'), parts along dimension 0, may hold values from -120 to 120
- norm_gain: float32 [6144], P('row'), may hold values from 0.25 to 1.75
- qkv_weight: bfloat16 [6144, 3, 3072], P('row', None, 'col'), may hold values from -2.5 to 2.5
- out_weight: bfloat16 [3072, 6144], P('col', 'row'), may hold values from -0.109375 to 0.109375
Outputs:
- projected: bfloat16 [1536, 6144], P('dp', 'row'), parts along dimension 0
There are 4 independent parts, one for each index of `dp`. A program takes and returns all parts, laid end to end along the dimension named above; an argument that names none is the same for every part. Nothing has to cross between parts.
All inputs are finite; a program needn't handle non-finite values.
Results may differ from a plain program's by a relative error of at most 0.025.
Values may be sent and summed in bfloat16 or wider, within the bound.
A program may use at most 64 MiB of HBM per device.

v0:
```python
import math

import jax
import jax.numpy as jnp
from jax import lax
from jax.sharding import PartitionSpec as P

K = 128


EPSILON = 1e-05


def attend(queries, key_rows, value_rows):
    query_total = queries.shape[0]
    head_count = queries.shape[1] // K
    scaling = 1.0 / math.sqrt(K)
    split_keys = key_rows.reshape(key_rows.shape[0], head_count, K)
    split_values = value_rows.reshape(value_rows.shape[0], head_count, K)
    split_queries = queries.reshape(query_total, head_count, K)
    scores = (
        jnp.einsum("qhd,khd->hqk", split_queries, split_keys, preferred_element_type=jnp.float32)
        * scaling
    )
    largest = jnp.max(scores, axis=2, keepdims=True)
    exponent = jnp.exp(scores - largest)
    softmax_weights = (exponent / jnp.sum(exponent, axis=2, keepdims=True)).astype(jnp.bfloat16)
    mixed = jnp.einsum(
        "hqk,khd->qhd", softmax_weights, split_values, preferred_element_type=jnp.float32
    )
    result = mixed.astype(jnp.bfloat16)
    return result.reshape(query_total, head_count * K)


def shards(tokens, norm_gain, qkv_weight, out_weight):
    row_count, block_width = tokens.shape
    full_width = block_width * lax.axis_size("row")
    values = tokens.astype(jnp.float32)
    totals, squares = lax.psum(
        (jnp.sum(values, axis=1, keepdims=True), jnp.sum(values * values, axis=1, keepdims=True)),
        "row",
    )
    average = totals / full_width
    variance = squares / full_width - average * average
    centered = values - average
    normed = (centered * lax.rsqrt(variance + EPSILON) * norm_gain).astype(jnp.bfloat16)
    head_columns = qkv_weight.shape[2]
    partial_value = jnp.dot(
        normed,
        qkv_weight.reshape(block_width, 3 * head_columns),
        preferred_element_type=jnp.float32,
    )
    summed = lax.psum(partial_value.astype(jnp.bfloat16), "row").reshape(row_count, 3, head_columns)
    attended = attend(summed[:, 0], summed[:, 1], summed[:, 2])
    partial_out = jnp.dot(attended, out_weight, preferred_element_type=jnp.float32)
    return lax.psum(partial_out.astype(jnp.bfloat16), "col")


def solution(mesh):
    in_specs = (P("dp", "row"), P("row"), P("row", None, "col"), P("col", "row"))
    out_specs = P("dp", "row")
    return jax.shard_map(shards, mesh=mesh, in_specs=in_specs, out_specs=out_specs, check_vma=False)
```

profile of v0, /device:TPU:0, one launch (start us, length us, event | category | flops | bytes accessed | tf_op | source)
XLA Modules:
  0.0 253.6 jit_solution(16139016888201354875)
XLA Ops:
  6.5 0.0 all-reduce.4.cloned.1.call-start
  6.5 1.7 convert_reduce_fusion
  8.3 0.0 copy-start
  8.3 18.6 %copy.7 = bf16[1536,3,1536]{0,2,1:T(8,128)(2,1)} copy(bf16[1536,3,1536]{2,0,1:T(8,128)(2,1)} %param.6) | data formatting | bytes 28311552 | tf_op args[2]
  26.9 13.5 %all-reduce = (f32[384,1]{0,1:T(1,128)S(1)}, f32[384,1]{0,1:T(1,128)S(1)}) all-reduce(f32[384,1]{0,1:T(1,128)S(1)} %broadcast_in_dim.4, f32[384,1]{0,1:T(1,128)S(1)} %broadcast_in_dim.10), channel_id=1, replica_groups=mesh['row'=4,'col'=2,'dp'=4] {'row'}, use_global_device_ids=true, to_apply=%region_1.0 | all-reduce | flops 768 | bytes 6144 | tf_op jit(solution)/shard_map/psum | solution.py:39
  40.4 0.0 copy-done
  40.4 9.4 %convolution_convert_fusion = bf16[384,4608]{1,0:T(8,128)(2,1)S(1)} fusion(bf16[1536,4608]{0,1:T(8,128)(2,1)} %bitcast.16, bf16[384,1536]{1,0:T(8,128)(2,1)} %param.4, f32[1536]{0:T(1024)S(1)} %copy-done, f32[384]{0:T(512)S(1)} %get-tuple-element.8, f32[384]{0:T(512)S(1)} %get-tuple-element.7), kind=kOutput, calls=%fused_computation.3 | convolution fusion | flops 5440536576 | bytes 18883584 | tf_op jit(solution)/shard_map/dot_general | solution.py:48
  49.9 3.6 %copy.8 = bf16[384,4608]{0,1:T(8,128)(2,1)} copy(bf16[384,4608]{1,0:T(8,128)(2,1)S(1)} %convolution_convert_fusion) | data formatting | bytes 7077888 | tf_op jit(solution)/shard_map/convert_element_type | solution.py:53
  53.5 0.0 all-reduce.4.cloned.1.call-update
  53.5 0.0 all-reduce.6.cloned.1.call-start
  53.6 132.1 %all-reduce.4.cloned.1.call-done = bf16[384,3,1536]{0,2,1:T(8,128)(2,1)} async-done(((bf16[384,3,1536]{0,2,1:T(8,128)(2,1)}), bf16[384,3,1536]{0,2,1:T(8,128)(2,1)}) %all-reduce.4.cloned.1.call-update) | async-done | bytes 3538960 | tf_op jit(solution)/shard_map/psum | solution.py:53
  185.7 2.3 fusion.18
  188.0 4.9 %fusion.19 = (f32[12,384]{1,0:T(8,128)}, f32[12,384,384]{1,2,0:T(8,128)}) fusion(bf16[384,12,128]{0,2,1:T(8,128)(2,1)S(1)} %bitcast.20, bf16[384,12,128]{0,2,1:T(8,128)(2,1)S(1)} %bitcast.19), kind=kOutput, calls=%fused_computation.25 | convolution fusion | flops 458293632 | bytes 9455616 | tf_op jit(solution)/shard_map/sub | solution.py:26
  192.9 4.0 %fusion.10 = bf16[12,128,384]{2,1,0:T(8,128)(2,1)S(1)} fusion(bf16[384,12,128]{0,2,1:T(8,128)(2,1)S(1)} %bitcast.18, f32[12,384,384]{1,2,0:T(8,128)} %get-tuple-element.15, f32[12,384]{1,0:T(8,128)} %get-tuple-element.14), kind=kOutput, calls=%fused_computation.16 | convolution fusion | flops 457113600 | bytes 9455616 | tf_op jit(solution)/shard_map/hqk,khd->qhd/dot_general | solution.py:28
  196.9 5.4 %convolution_convert_fusion.1 = bf16[384,1536]{1,0:T(8,128)(2,1)} fusion(bf16[384,1536]{0,1:T(8,128)(2,1)S(1)} %bitcast.21, bf16[1536,1536]{1,0:T(8,128)(2,1)} %param.7), kind=kOutput, calls=%fused_computation.11 | convolution fusion | flops 1812529152 | bytes 7077888 | tf_op jit(solution)/shard_map/dot_general | solution.py:55
  202.3 0.0 all-reduce.6.cloned.1.call-update
  202.3 42.1 %all-reduce.6.cloned.1.call-done = bf16[384,1536]{1,0:T(8,128)(2,1)} async-done(((bf16[384,1536]{1,0:T(8,128)(2,1)}), bf16[384,1536]{1,0:T(8,128)(2,1)}) %all-reduce.6.cloned.1.call-update) | async-done | bytes 1179664 | tf_op jit(solution)/shard_map/psum | solution.py:56
  244.4 2.4 copy.17
  (3 shorter events, 0.0 us)
Async XLA Ops:
  6.5 179.1 %all-reduce.4.cloned.1.call-start = ((), (), s32[]{:S(2)}) async-start(), calls=%async_computation | async-start | bytes 7077888 | tf_op jit(solution)/shard_map/psum | solution.py:53
  8.3 32.1 %copy-start = (f32[1536]{0:T(1024)S(1)}, f32[1536]{0:T(1024)}, u32[]{:S(2)}) copy-start(f32[1536]{0:T(1024)} %param.5) | copy-start | bytes 18436
  53.5 190.9 %all-reduce.6.cloned.1.call-start = ((), (), s32[]{:S(2)}) async-start(), calls=%async_computation.1 | async-start | bytes 2359296 | tf_op jit(solution)/shard_map/psum | solution.py:56
Sparse Core Ops, SparseCore 0:
  53.6 131.9 all-reduce.3
  202.4 41.9 all-reduce.5
where the time goes:
time: 254 us
  waiting for transfers between devices  174 us (69%)
  local copies, waits for them, and re-layouts  27 us (11%)
  matrix products  23.7 us (9%)
  blocking collectives  13.5 us (5%)
  between operations  13.4 us (5%)
    psum x1, waiting for transfers between devices, shards(): lax.psum(partial_value.astype(jnp.bfloat16), 'row')  132 us
    psum x1, waiting for transfers between devices, shards(): return lax.psum(partial_out.astype(jnp.bfloat16), 'col')  42.1 us
    unnamed x4, local copies, waits for them, and re-layouts  21 us
    psum x1, blocking collectives, shards(): lax.psum((jnp.sum(values, axis=1, keepdims=True), jnp.sum(values * values...  13.5 us
    dot_general x1, matrix products, shards(): jnp.dot(normed, qkv_weight.reshape(block_width, 3 * head_columns), prefer...  9.45 us
    dot_general x1, matrix products, shards(): jnp.dot(attended, out_weight, preferred_element_type=jnp.float32)  5.37 us
  transfers between devices with their start and end apart: 2, of which 2 were waited for; matrix products, arithmetic and copies ran while one was open for 0% of the time, Pallas kernels for 0%

commit v1 on v0

--- a/solution.py
+++ b/solution.py
@@ -1,8 +1,11 @@
+import functools
 import math
 
 import jax
 import jax.numpy as jnp
 from jax import lax
+from jax.experimental import pallas as pl
+from jax.experimental.pallas import tpu as pltpu
 from jax.sharding import PartitionSpec as P
 
 K = 128
@@ -56,7 +59,285 @@
     return lax.psum(partial_out.astype(jnp.bfloat16), "col")
 
 
+MESH = pl.DeviceIdType.MESH
+WIDE = 2 * K
+SKEW = 2
+ROWS = 32
+
+
+def sublayer_kernel(
+    rows_n, cols_n, tok_hbm, gain_ref, w_hbm, wo_hbm, out_ref,
+    tok, wide_w, out_w, stat_col, stats, normed, arrived, summed, attended, mine, theirs,
+    tok_sem, w_sem, wo_sem, st_send, st_recv, rs_send, rs_recv, at_send, at_recv, x_send, x_recv,
+):
+    z = lax.axis_index("row")
+    col = lax.axis_index("col")
+    tokens_n, block = tok.shape
+    half = w_hbm.shape[2] // 2
+    pairs = half // WIDE
+    chunks = 3 * pairs
+    tiles = block // WIDE
+    scaling = 1.0 / math.sqrt(K)
+
+    def weight_copy(d, c):
+        pair, kind = c // 3, c % 3
+        first = pl.multiple_of(d * half + pair * WIDE, WIDE)
+        return pltpu.make_async_copy(
+            w_hbm.at[kind, :, pl.ds(first, WIDE)], wide_w.at[d, c], w_sem.at[d, c]
+        )
+
+    tok_copy = pltpu.make_async_copy(tok_hbm, tok, tok_sem)
+    tok_copy.start()
+
+    @pl.loop(0, chunks)
+    def _(c):
+        weight_copy(0, c).start()
+        weight_copy(1, c).start()
+
+    wo_copy = pltpu.make_async_copy(wo_hbm, out_w, wo_sem)
+    wo_copy.start()
+
+    barrier = pltpu.get_barrier_semaphore()
+    for o in range(1, rows_n):
+        pl.semaphore_signal(
+            barrier, inc=1, device_id={"row": lax.rem(z + o, rows_n)}, device_id_type=MESH
+        )
+    pl.semaphore_signal(barrier, inc=1, device_id={"col": 1 - col}, device_id_type=MESH)
+
+    tok_copy.wait()
+
+    @pl.loop(0, tokens_n // ROWS)
+    def _(i):
+        at = pl.ds(pl.multiple_of(i * ROWS, ROWS), ROWS)
+        x = tok[at, :].astype(jnp.float32)
+        mean = jnp.sum(x, axis=1, keepdims=True) * (1.0 / block)
+        away = x - mean
+        square = jnp.sum(away * away, axis=1, keepdims=True)
+        stat_col[0, at, :] = jnp.broadcast_to(mean, (ROWS, 128))
+        stat_col[1, at, :] = jnp.broadcast_to(square, (ROWS, 128))
+
+    stats[z, 0] = stat_col[0].T[0:8]
+    stats[z, 1] = stat_col[1].T[0:8]
+    pl.semaphore_wait(barrier, rows_n)
+
+    def stat_copy(o):
+        return pltpu.make_async_remote_copy(
+            src_ref=stats.at[z], dst_ref=stats.at[z], send_sem=st_send.at[o],
+            recv_sem=st_recv.at[z], device_id={"row": lax.rem(z + o, rows_n)},
+            device_id_type=MESH,
+        )
+
+    def stat_arrival(o):
+        source = lax.rem(z + o, rows_n)
+        return pltpu.make_async_remote_copy(
+            src_ref=stats.at[source], dst_ref=stats.at[source], send_sem=st_send.at[o],
+            recv_sem=st_recv.at[source], device_id={"row": source}, device_id_type=MESH,
+        )
+
+    for o in range(1, rows_n):
+        stat_copy(o).start()
+    for o in range(1, rows_n):
+        stat_arrival(o).wait_recv()
+    mean = sum(stats[i, 0] for i in range(rows_n)) * (1.0 / rows_n)
+    spread = sum(
+        stats[i, 1] * (1.0 / block) + (stats[i, 0] - mean) * (stats[i, 0] - mean)
+        for i in range(rows_n)
+    ) * (1.0 / rows_n)
+    scale = lax.rsqrt(spread + EPSILON)
+    stat_col[0] = jnp.broadcast_to(mean[0:1], (128, tokens_n)).T
+    stat_col[1] = jnp.broadcast_to(scale[0:1], (128, tokens_n)).T
+
+    @pl.loop(0, tokens_n // ROWS)
+    def _(i):
+        at = pl.ds(pl.multiple_of(i * ROWS, ROWS), ROWS)
+        x = tok[at, :].astype(jnp.float32)
+        away = (x - stat_col[0, at, 0:1]) * stat_col[1, at, 0:1]
+        normed[at, :] = (away * gain_ref[...]).astype(jnp.bfloat16)
+
+    def place(d):
+        return z if d == 1 else rows_n - 1 - z
+
+    def onward(d):
+        return {"row": jnp.clip(z + 1 if d == 1 else z - 1, 0, rows_n - 1)}
+
+    def back(d):
+        return {"row": jnp.clip(z - 1 if d == 1 else z + 1, 0, rows_n - 1)}
+
+    def sum_copy(d, c):
+        return pltpu.make_async_remote_copy(
+            src_ref=summed.at[d, c], dst_ref=arrived.at[d, c], send_sem=rs_send.at[d, c],
+            recv_sem=rs_recv.at[d, c], device_id=onward(d), device_id_type=MESH,
+        )
+
+    def attended_copy(d, p):
+        return pltpu.make_async_remote_copy(
+            src_ref=attended.at[d, p], dst_ref=attended.at[d, p], send_sem=at_send.at[d, p],
+            recv_sem=at_recv.at[d, p], device_id=back(d), device_id_type=MESH,
+        )
+
+    def attend_pair(d, p):
+        for h in range(2):
+            at = slice(h * K, (h + 1) * K)
+            q, k, v = (summed[d, 3 * p + kind, :, at] for kind in range(3))
+            scores = lax.dot_general(
+                q, k, (((1,), (1,)), ((), ())), preferred_element_type=jnp.float32
+            ) * scaling
+            exponent = jnp.exp(scores - jnp.max(scores, axis=1, keepdims=True))
+            weights = exponent / jnp.sum(exponent, axis=1, keepdims=True)
+            attended[d, p, :, at] = jnp.dot(
+                weights.astype(jnp.bfloat16), v, preferred_element_type=jnp.float32
+            ).astype(jnp.bfloat16)
+
+    last_place = rows_n - 1
+    slots = chunks + 2 * SKEW * last_place
+
+    @pl.loop(0, slots)
+    def _(t):
+        for d in range(2):
+            pos = place(d)
+            c = t - SKEW * pos
+
+            @pl.when((c >= 0) & (c < chunks))
+            def _():
+                weight_copy(d, c).wait()
+                part = jnp.dot(normed[...], wide_w[d, c], preferred_element_type=jnp.float32)
+
+                @pl.when(pos == 0)
+                def _():
+                    summed[d, c] = part.astype(jnp.bfloat16)
+
+                @pl.when(pos > 0)
+                def _():
+                    sum_copy(d, c).wait_recv()
+                    total = part + arrived[d, c].astype(jnp.float32)
+                    summed[d, c] = total.astype(jnp.bfloat16)
+
+                @pl.when(pos < last_place)
+                def _():
+                    sum_copy(d, c).start()
+
+        for d in range(2):
+            pos = place(d)
+            e = t - SKEW * last_place - SKEW * (last_place - pos)
+            p = e // 3
+
+            @pl.when((e >= 0) & (e < chunks) & (e % 3 == 2))
+            def _():
+                @pl.when(pos == last_place)
+                def _():
+                    attend_pair(d, p)
+
+                @pl.when(pos < last_place)
+                def _():
+                    attended_copy(d, p).wait_recv()
+
+                @pl.when(pos > 0)
+                def _():
+                    attended_copy(d, p).start()
+
+    wo_copy.wait()
+
+    def exchange(j):
+        return pltpu.make_async_remote_copy(
+            src_ref=mine.at[j], dst_ref=theirs.at[j], send_sem=x_send.at[j],
+            recv_sem=x_recv.at[j], device_id={"col": 1 - col}, device_id_type=MESH,
+        )
+
+    @pl.loop(0, tiles)
+    def _(j):
+        at = pl.ds(pl.multiple_of(j * WIDE, WIDE), WIDE)
+        total = jnp.zeros((tokens_n, WIDE), jnp.float32)
+        for d in range(2):
+            for p in range(pairs):
+                first = d * half + p * WIDE
+                total = total + jnp.dot(
+                    attended[d, p], out_w[first:first + WIDE, at],
+                    preferred_element_type=jnp.float32,
+                )
+        mine[j] = total.astype(jnp.bfloat16)
+        exchange(j).start()
+
+    @pl.loop(0, tiles)
+    def _(j):
+        at = pl.ds(pl.multiple_of(j * WIDE, WIDE), WIDE)
+        exchange(j).wait_recv()
+        both = mine[j].astype(jnp.float32) + theirs[j].astype(jnp.float32)
+        out_ref[:, at] = both.astype(jnp.bfloat16)
+
+    for o in range(1, rows_n):
+        stat_copy(o).wait_send()
+    for d in range(2):
+        pos = place(d)
+
+        @pl.when(pos < last_place)
+        def _():
+            @pl.loop(0, chunks)
+            def _(c):
+                sum_copy(d, c).wait_send()
+
+        @pl.when(pos > 0)
+        def _():
+            @pl.loop(0, pairs)
+            def _(p):
+                attended_copy(d, p).wait_send()
+
+    @pl.loop(0, tiles)
+    def _(j):
+        exchange(j).wait_send()
+
+
+def fused_shards(rows_n, cols_n, tokens, norm_gain, qkv_weight, out_weight):
+    tokens_n, block = tokens.shape
+    head_columns = qkv_weight.shape[2]
+    pairs = head_columns // (2 * WIDE)
+    chunks = 3 * pairs
+    tiles = block // WIDE
+    any_space = pl.BlockSpec(memory_space=pl.ANY)
+    vmem = pl.BlockSpec(memory_space=pltpu.VMEM)
+    dma = pltpu.SemaphoreType.DMA
+    bf16, f32 = jnp.bfloat16, jnp.float32
+    return pl.pallas_call(
+        functools.partial(sublayer_kernel, rows_n, cols_n),
+        out_shape=jax.ShapeDtypeStruct((tokens_n, block), bf16),
+        in_specs=[any_space, vmem, any_space, any_space],
+        out_specs=vmem,
+        scratch_shapes=[
+            pltpu.VMEM((tokens_n, block), bf16),
+            pltpu.VMEM((2, chunks, block, WIDE), bf16),
+            pltpu.VMEM((head_columns, block), bf16),
+            pltpu.VMEM((2, tokens_n, 128), f32),
+            pltpu.VMEM((rows_n, 2, 8, tokens_n), f32),
+            pltpu.VMEM((tokens_n, block), bf16),
+            pltpu.VMEM((2, chunks, tokens_n, WIDE), bf16),
+            pltpu.VMEM((2, chunks, tokens_n, WIDE), bf16),
+            pltpu.VMEM((2, pairs, tokens_n, WIDE), bf16),
+            pltpu.VMEM((tiles, tokens_n, WIDE), bf16),
+            pltpu.VMEM((tiles, tokens_n, WIDE), bf16),
+            dma, dma((2, chunks)), dma,
+            dma((rows_n,)), dma((rows_n,)),
+            dma((2, chunks)), dma((2, chunks)),
+            dma((2, pairs)), dma((2, pairs)),
+            dma((tiles,)), dma((tiles,)),
+        ],
+        compiler_params=pltpu.CompilerParams(
+            collective_id=0, has_side_effects=True, vmem_limit_bytes=60 * 1024 * 1024
+        ),
+    )(tokens, norm_gain.reshape(1, block), jnp.transpose(qkv_weight, (1, 0, 2)), out_weight)
+
+
 def solution(mesh):
     in_specs = (P("dp", "row"), P("row"), P("row", None, "col"), P("col", "row"))
     out_specs = P("dp", "row")
-    return jax.shard_map(shards, mesh=mesh, in_specs=in_specs, out_specs=out_specs, check_vma=False)
+    rows_n, cols_n = mesh.shape["row"], mesh.shape["col"]
+
+    def body(tokens, norm_gain, qkv_weight, out_weight):
+        tokens_n, block = tokens.shape
+        fits = (
+            cols_n == 2 and rows_n >= 2 and qkv_weight.shape[2] % (2 * WIDE) == 0
+            and block % WIDE == 0 and tokens_n % 128 == 0
+        )
+        if fits:
+            return fused_shards(rows_n, cols_n, tokens, norm_gain, qkv_weight, out_weight)
+        return shards(tokens, norm_gain, qkv_weight, out_weight)
+
+    return jax.shard_map(body, mesh=mesh, in_specs=in_specs, out_specs=out_specs, check_vma=False)

time: 254 us -> 115 us (0.45)
  waiting for transfers between devices: 174 us -> 0 us
  Pallas kernels: 0 us -> 111 us
  matrix products: 23.7 us -> 0 us
  local copies, waits for them, and re-layouts: 27 us -> 3.65 us
  blocking collectives: 13.5 us -> 0 us
  between operations: 13.4 us -> 0.01 us
    psum x2 -> x0, waiting for transfers between devices: 174 us -> none  [the longest x1 132 us: shards(): lax.psum(partial_value.astype(jnp.bfloat16), 'row')]
    pallas_call x0 -> x1, Pallas kernels: none -> 111 us  [fused_shards(): pl.pallas_call(functools.partial(sublayer_kernel, rows_n, cols_n), out_sh...]
    dot_general x3 -> x0, matrix products: 18.8 us -> none  [the longest x1 9.45 us: shards(): jnp.dot(normed, qkv_weight.reshape(block_width, 3 * head_columns), prefer...]
    unnamed x4 -> x1, local copies, waits for them, and re-layouts: 21 us -> 2.36 us
    psum x1 -> x0, blocking collectives: 13.5 us -> none  [shards(): lax.psum((jnp.sum(values, axis=1, keepdims=True), jnp.sum(values * values...]
    sub x1 -> x0, matrix products: 4.9 us -> none  [attend(): exponent = jnp.exp(scores - largest)]
    convert_element_type x1 -> x0, local copies, waits for them, and re-layouts: 3.61 us -> none  [shards(): partial_value.astype(jnp.bfloat16)]
  transfers between devices with their start and end apart: 2 -> 0, of which waited for: 2 -> 0; matrix products, arithmetic and copies ran while one was open for 0% -> 0% of each run, Pallas kernels for 0% -> 0%
where the time goes in v1:
time: 115 us
  Pallas kernels  111 us (97%)
  local copies, waits for them, and re-layouts  3.65 us (3%)
    pallas_call x1, Pallas kernels, fused_shards(): pl.pallas_call(functools.partial(sublayer_kernel, rows_n, cols_n), out_sh...  111 us
    unnamed x1, local copies, waits for them, and re-layouts  2.36 us

profile of v1, /device:TPU:0, one launch (start us, length us, event | category | flops | bytes accessed | tf_op | source)
XLA Modules:
  0.0 115.0 jit_solution(18188421257376544116)
XLA Ops:
  0.0 1.3 %reshape.3.gain_ref = f32[1,1536]{1,0:T(1,128)} reshape(f32[1536]{0:T(1024)} %param.5) | data formatting | bytes 12288 | tf_op jit(solution)/shard_map/reshape | solution.py:325
  1.3 111.4 %shard_map.46 = bf16[384,1536]{1,0:T(8,128)(2,1)} custom-call(bf16[384,1536]{1,0:T(8,128)(2,1)} %tok_hbm.1, f32[1,1536]{1,0:T(1,128)} %reshape.3.gain_ref, bf16[3,1536,1536]{2,1,0:T(8,128)(2,1)} %bitcast.1, bf16[1536,1536]{1,0:T(8,128)(2,1)} %wo_hbm.1), custom_call_target="tpu_custom_call" | custom-call | tf_op jit(solution)/shard_map/pallas_call | solution.py:299
  112.7 2.4 %copy.6 = bf16[384,1536]{1,0:T(8,128)(2,1)} copy(bf16[384,1536]{1,0:T(8,128)(2,1)} %shard_map.46) | data formatting | bytes 2359296

commit v2 on v1

--- a/solution.py
+++ b/solution.py
@@ -63,12 +63,15 @@
 WIDE = 2 * K
 SKEW = 2
 ROWS = 32
+PIECE = 128
+PARTS = 2
 
 
 def sublayer_kernel(
     rows_n, cols_n, tok_hbm, gain_ref, w_hbm, wo_hbm, out_ref,
-    tok, wide_w, out_w, stat_col, stats, normed, arrived, summed, attended, mine, theirs,
-    tok_sem, w_sem, wo_sem, st_send, st_recv, rs_send, rs_recv, at_send, at_recv, x_send, x_recv,
+    tok, wide_w, out_w, stat_col, stats, normed, arrived, summed, attended, late_w, early,
+    tok_sem, w_sem, wo_sem, late_sem, st_send, st_recv, rs_send, rs_recv, at_send, at_recv,
+    x_send, x_recv, lw_send, lw_recv, la_send, la_recv,
 ):
     z = lax.axis_index("row")
     col = lax.axis_index("col")
@@ -77,6 +80,9 @@
     pairs = half // WIDE
     chunks = 3 * pairs
     tiles = block // WIDE
+    pieces = tokens_n // PIECE
+    part_rows = tokens_n // PARTS
+    partner = {"col": 1 - col}
     scaling = 1.0 / math.sqrt(K)
 
     def weight_copy(d, c):
@@ -97,12 +103,33 @@
     wo_copy = pltpu.make_async_copy(wo_hbm, out_w, wo_sem)
     wo_copy.start()
 
+    def late_rows(d):
+        return wo_hbm.at[pl.ds(d * half + (pairs - 1) * WIDE, WIDE)]
+
+    def late_copy(d):
+        return pltpu.make_async_copy(late_rows(d), late_w.at[col, d], late_sem.at[d])
+
+    def late_share(d):
+        return pltpu.make_async_remote_copy(
+            src_ref=late_rows(d), dst_ref=late_w.at[col, d], send_sem=lw_send.at[d],
+            recv_sem=lw_recv.at[d], device_id=partner, device_id_type=MESH,
+        )
+
+    def late_arrival(d):
+        return pltpu.make_async_remote_copy(
+            src_ref=late_rows(d), dst_ref=late_w.at[1 - col, d], send_sem=lw_send.at[d],
+            recv_sem=lw_recv.at[d], device_id=partner, device_id_type=MESH,
+        )
+
+    for d in range(2):
+        late_copy(d).start()
+
     barrier = pltpu.get_barrier_semaphore()
     for o in range(1, rows_n):
         pl.semaphore_signal(
             barrier, inc=1, device_id={"row": lax.rem(z + o, rows_n)}, device_id_type=MESH
         )
-    pl.semaphore_signal(barrier, inc=1, device_id={"col": 1 - col}, device_id_type=MESH)
+    pl.semaphore_signal(barrier, inc=1, device_id=partner, device_id_type=MESH)
 
     tok_copy.wait()
 
@@ -136,6 +163,8 @@
 
     for o in range(1, rows_n):
         stat_copy(o).start()
+    for d in range(2):
+        late_share(d).start()
     for o in range(1, rows_n):
         stat_arrival(o).wait_recv()
     mean = sum(stats[i, 0] for i in range(rows_n)) * (1.0 / rows_n)
@@ -163,33 +192,69 @@
     def back(d):
         return {"row": jnp.clip(z - 1 if d == 1 else z + 1, 0, rows_n - 1)}
 
-    def sum_copy(d, c):
-        return pltpu.make_async_remote_copy(
-            src_ref=summed.at[d, c], dst_ref=arrived.at[d, c], send_sem=rs_send.at[d, c],
-            recv_sem=rs_recv.at[d, c], device_id=onward(d), device_id_type=MESH,
-        )
-
-    def attended_copy(d, p):
-        return pltpu.make_async_remote_copy(
-            src_ref=attended.at[d, p], dst_ref=attended.at[d, p], send_sem=at_send.at[d, p],
-            recv_sem=at_recv.at[d, p], device_id=back(d), device_id_type=MESH,
-        )
-
-    def attend_pair(d, p):
+    def sum_copy(d, c, i):
+        at = pl.ds(i * part_rows, part_rows)
+        return pltpu.make_async_remote_copy(
+            src_ref=summed.at[d, c, at], dst_ref=arrived.at[d, c, at],
+            send_sem=rs_send.at[d, c, i], recv_sem=rs_recv.at[d, c, i],
+            device_id=onward(d), device_id_type=MESH,
+        )
+
+    def attended_copy(d, p, i):
+        piece = attended.at[col, d, p, pl.ds(i * PIECE, PIECE)]
+        return pltpu.make_async_remote_copy(
+            src_ref=piece, dst_ref=piece, send_sem=at_send.at[d, p, i],
+            recv_sem=at_recv.at[d, p, i], device_id=back(d), device_id_type=MESH,
+        )
+
+    def cross_copy(d, i, owner):
+        piece = attended.at[owner, d, pairs - 1, pl.ds(i * PIECE, PIECE)]
+        return pltpu.make_async_remote_copy(
+            src_ref=piece, dst_ref=piece, send_sem=la_send.at[d, i],
+            recv_sem=la_recv.at[d, i], device_id=partner, device_id_type=MESH,
+        )
+
+    def exchange(j, owner):
+        return pltpu.make_async_remote_copy(
+            src_ref=early.at[owner, j], dst_ref=early.at[owner, j], send_sem=x_send.at[j],
+            recv_sem=x_recv.at[j], device_id=partner, device_id_type=MESH,
+        )
+
+    def attend_piece(d, p, i):
+        rows = pl.ds(i * PIECE, PIECE)
         for h in range(2):
             at = slice(h * K, (h + 1) * K)
-            q, k, v = (summed[d, 3 * p + kind, :, at] for kind in range(3))
+            q = summed[d, 3 * p, rows, at]
+            k = summed[d, 3 * p + 1, :, at]
+            v = summed[d, 3 * p + 2, :, at]
             scores = lax.dot_general(
                 q, k, (((1,), (1,)), ((), ())), preferred_element_type=jnp.float32
             ) * scaling
             exponent = jnp.exp(scores - jnp.max(scores, axis=1, keepdims=True))
             weights = exponent / jnp.sum(exponent, axis=1, keepdims=True)
-            attended[d, p, :, at] = jnp.dot(
+            attended[col, d, p, rows, at] = jnp.dot(
                 weights.astype(jnp.bfloat16), v, preferred_element_type=jnp.float32
             ).astype(jnp.bfloat16)
 
+    def project_early():
+        @pl.loop(0, tiles)
+        def _(j):
+            at = pl.ds(pl.multiple_of(j * WIDE, WIDE), WIDE)
+            total = jnp.zeros((tokens_n, WIDE), jnp.float32)
+            for d in range(2):
+                for p in range(pairs - 1):
+                    first = d * half + p * WIDE
+                    total = total + jnp.dot(
+                        attended[col, d, p], out_w[first:first + WIDE, at],
+                        preferred_element_type=jnp.float32,
+                    )
+            early[col, j] = total.astype(jnp.bfloat16)
+            exchange(j, col).start()
+
     last_place = rows_n - 1
     slots = chunks + 2 * SKEW * last_place
+    early_slot = chunks - 4 + SKEW * (last_place + jnp.maximum(z, last_place - z))
+    wo_copy.wait()
 
     @pl.loop(0, slots)
     def _(t):
@@ -202,19 +267,24 @@
                 weight_copy(d, c).wait()
                 part = jnp.dot(normed[...], wide_w[d, c], preferred_element_type=jnp.float32)
 
-                @pl.when(pos == 0)
-                def _():
-                    summed[d, c] = part.astype(jnp.bfloat16)
-
-                @pl.when(pos > 0)
-                def _():
-                    sum_copy(d, c).wait_recv()
-                    total = part + arrived[d, c].astype(jnp.float32)
-                    summed[d, c] = total.astype(jnp.bfloat16)
-
-                @pl.when(pos < last_place)
-                def _():
-                    sum_copy(d, c).start()
+                for i in range(PARTS):
+                    lo = i * part_rows
+                    at = pl.ds(lo, part_rows)
+                    share = part[lo:lo + part_rows]
+
+                    @pl.when(pos == 0)
+                    def _():
+                        summed[d, c, at] = share.astype(jnp.bfloat16)
+
+                    @pl.when(pos > 0)
+                    def _():
+                        sum_copy(d, c, i).wait_recv()
+                        total = share + arrived[d, c, at].astype(jnp.float32)
+                        summed[d, c, at] = total.astype(jnp.bfloat16)
+
+                    @pl.when(pos < last_place)
+                    def _():
+                        sum_copy(d, c, i).start()
 
         for d in range(2):
             pos = place(d)
@@ -223,46 +293,45 @@
 
             @pl.when((e >= 0) & (e < chunks) & (e % 3 == 2))
             def _():
-                @pl.when(pos == last_place)
-                def _():
-                    attend_pair(d, p)
-
-                @pl.when(pos < last_place)
-                def _():
-                    attended_copy(d, p).wait_recv()
-
-                @pl.when(pos > 0)
-                def _():
-                    attended_copy(d, p).start()
-
-    wo_copy.wait()
-
-    def exchange(j):
-        return pltpu.make_async_remote_copy(
-            src_ref=mine.at[j], dst_ref=theirs.at[j], send_sem=x_send.at[j],
-            recv_sem=x_recv.at[j], device_id={"col": 1 - col}, device_id_type=MESH,
-        )
+                for i in range(pieces):
+                    @pl.when(pos == last_place)
+                    def _():
+                        attend_piece(d, p, i)
+
+                    @pl.when(pos < last_place)
+                    def _():
+                        attended_copy(d, p, i).wait_recv()
+
+                    @pl.when(pos > 0)
+                    def _():
+                        attended_copy(d, p, i).start()
+
+                    @pl.when(p == pairs - 1)
+                    def _():
+                        cross_copy(d, i, col).start()
+
+        @pl.when(t == early_slot)
+        def _():
+            project_early()
+
+    for d in range(2):
+        late_copy(d).wait()
+        late_arrival(d).wait_recv()
+        for i in range(pieces):
+            cross_copy(d, i, 1 - col).wait_recv()
 
     @pl.loop(0, tiles)
     def _(j):
         at = pl.ds(pl.multiple_of(j * WIDE, WIDE), WIDE)
-        total = jnp.zeros((tokens_n, WIDE), jnp.float32)
-        for d in range(2):
-            for p in range(pairs):
-                first = d * half + p * WIDE
+        exchange(j, 1 - col).wait_recv()
+        total = early[0, j].astype(jnp.float32) + early[1, j].astype(jnp.float32)
+        for owner in range(2):
+            for d in range(2):
                 total = total + jnp.dot(
-                    attended[d, p], out_w[first:first + WIDE, at],
+                    attended[owner, d, pairs - 1], late_w[owner, d, :, at],
                     preferred_element_type=jnp.float32,
                 )
-        mine[j] = total.astype(jnp.bfloat16)
-        exchange(j).start()
-
-    @pl.loop(0, tiles)
-    def _(j):
-        at = pl.ds(pl.multiple_of(j * WIDE, WIDE), WIDE)
-        exchange(j).wait_recv()
-        both = mine[j].astype(jnp.float32) + theirs[j].astype(jnp.float32)
-        out_ref[:, at] = both.astype(jnp.bfloat16)
+        out_ref[:, at] = total.astype(jnp.bfloat16)
 
     for o in range(1, rows_n):
         stat_copy(o).wait_send()
@@ -273,17 +342,24 @@
         def _():
             @pl.loop(0, chunks)
             def _(c):
-                sum_copy(d, c).wait_send()
+                for i in range(PARTS):
+                    sum_copy(d, c, i).wait_send()
 
         @pl.when(pos > 0)
         def _():
             @pl.loop(0, pairs)
             def _(p):
-                attended_copy(d, p).wait_send()
+                for i in range(pieces):
+                    attended_copy(d, p, i).wait_send()
 
     @pl.loop(0, tiles)
     def _(j):
-        exchange(j).wait_send()
+        exchange(j, col).wait_send()
+
+    for d in range(2):
+        late_share(d).wait_send()
+        for i in range(pieces):
+            cross_copy(d, i, col).wait_send()
 
 
 def fused_shards(rows_n, cols_n, tokens, norm_gain, qkv_weight, out_weight):
@@ -292,6 +368,7 @@
     pairs = head_columns // (2 * WIDE)
     chunks = 3 * pairs
     tiles = block // WIDE
+    pieces = tokens_n // PIECE
     any_space = pl.BlockSpec(memory_space=pl.ANY)
     vmem = pl.BlockSpec(memory_space=pltpu.VMEM)
     dma = pltpu.SemaphoreType.DMA
@@ -310,14 +387,15 @@
             pltpu.VMEM((tokens_n, block), bf16),
             pltpu.VMEM((2, chunks, tokens_n, WIDE), bf16),
             pltpu.VMEM((2, chunks, tokens_n, WIDE), bf16),
-            pltpu.VMEM((2, pairs, tokens_n, WIDE), bf16),
-            pltpu.VMEM((tiles, tokens_n, WIDE), bf16),
-            pltpu.VMEM((tiles, tokens_n, WIDE), bf16),
-            dma, dma((2, chunks)), dma,
+            pltpu.VMEM((2, 2, pairs, tokens_n, WIDE), bf16),
+            pltpu.VMEM((2, 2, WIDE, block), bf16),
+            pltpu.VMEM((2, tiles, tokens_n, WIDE), bf16),
+            dma, dma((2, chunks)), dma, dma((2,)),
             dma((rows_n,)), dma((rows_n,)),
-            dma((2, chunks)), dma((2, chunks)),
-            dma((2, pairs)), dma((2, pairs)),
-            dma((tiles,)), dma((tiles,)),
+            dma((2, chunks, PARTS)), dma((2, chunks, PARTS)),
+            dma((2, pairs, pieces)), dma((2, pairs, pieces)),
+            dma((tiles,)), dma((tiles,)), dma((2,)), dma((2,)),
+            dma((2, pieces)), dma((2, pieces)),
         ],
         compiler_params=pltpu.CompilerParams(
             collective_id=0, has_side_effects=True, vmem_limit_bytes=60 * 1024 * 1024
@@ -334,6 +412,7 @@
         tokens_n, block = tokens.shape
         fits = (
             cols_n == 2 and rows_n >= 2 and qkv_weight.shape[2] % (2 * WIDE) == 0
+            and qkv_weight.shape[2] >= 4 * WIDE
             and block % WIDE == 0 and tokens_n % 128 == 0
         )
         if fits:

time: 115 us -> 113 us (0.983)
  Pallas kernels: 111 us -> 109 us
    pallas_call x1, Pallas kernels: 111 us -> 109 us  [fused_shards(): pl.pallas_call(functools.partial(sublayer_kernel, rows_n, cols_n), out_sh...]
where the time goes in v2:
time: 113 us
  Pallas kernels  109 us (96%)
  local copies, waits for them, and re-layouts  3.65 us (3%)
    pallas_call x1, Pallas kernels, fused_shards(): pl.pallas_call(functools.partial(sublayer_kernel, rows_n, cols_n), out_sh...  109 us
    unnamed x1, local copies, waits for them, and re-layouts  2.36 us

profile of v2, /device:TPU:0, one launch (start us, length us, event | category | flops | bytes accessed | tf_op | source)
XLA Modules:
  0.0 113.0 jit_solution(1621127479477208382)
XLA Ops:
  0.0 1.3 %reshape.3.gain_ref = f32[1,1536]{1,0:T(1,128)} reshape(f32[1536]{0:T(1024)} %param.5) | data formatting | bytes 12288 | tf_op jit(solution)/shard_map/reshape | solution.py:403
  1.3 109.4 %shard_map.46 = bf16[384,1536]{1,0:T(8,128)(2,1)} custom-call(bf16[384,1536]{1,0:T(8,128)(2,1)} %tok_hbm.1, f32[1,1536]{1,0:T(1,128)} %reshape.3.gain_ref, bf16[3,1536,1536]{2,1,0:T(8,128)(2,1)} %bitcast.1, bf16[1536,1536]{1,0:T(8,128)(2,1)} %wo_hbm.1), custom_call_target="tpu_custom_call" | custom-call | tf_op jit(solution)/shard_map/pallas_call | solution.py:376
  110.7 2.4 %copy.6 = bf16[384,1536]{1,0:T(8,128)(2,1)} copy(bf16[384,1536]{1,0:T(8,128)(2,1)} %shard_map.46) | data formatting | bytes 2359296

commit v3 on v2

--- a/solution.py
+++ b/solution.py
@@ -61,7 +61,7 @@
 
 MESH = pl.DeviceIdType.MESH
 WIDE = 2 * K
-SKEW = 2
+SKEW = 1
 ROWS = 32
 PIECE = 128
 PARTS = 2
@@ -254,7 +254,6 @@
     last_place = rows_n - 1
     slots = chunks + 2 * SKEW * last_place
     early_slot = chunks - 4 + SKEW * (last_place + jnp.maximum(z, last_place - z))
-    wo_copy.wait()
 
     @pl.loop(0, slots)
     def _(t):
@@ -312,6 +311,7 @@
 
         @pl.when(t == early_slot)
         def _():
+            wo_copy.wait()
             project_early()
 
     for d in range(2):

time: 113 us -> 112 us (level)
    pallas_call x1, Pallas kernels: 109 us -> 108 us  [fused_shards(): pl.pallas_call(functools.partial(sublayer_kernel, rows_n, cols_n), out_sh...]
where the time goes in v3:
time: 112 us; the launch traced here: 111 us
  Pallas kernels  108 us (96%)
  local copies, waits for them, and re-layouts  3.65 us (3%)
    pallas_call x1, Pallas kernels, fused_shards(): pl.pallas_call(functools.partial(sublayer_kernel, rows_n, cols_n), out_sh...  108 us
    unnamed x1, local copies, waits for them, and re-layouts  2.36 us

profile of v3, /device:TPU:0, one launch (start us, length us, event | category | flops | bytes accessed | tf_op | source)
XLA Modules:
  0.0 111.5 jit_solution(2572136958724914401)
XLA Ops:
  0.0 1.3 %reshape.3.gain_ref = f32[1,1536]{1,0:T(1,128)} reshape(f32[1536]{0:T(1024)} %param.5) | data formatting | bytes 12288 | tf_op jit(solution)/shard_map/reshape | solution.py:403
  1.3 107.8 %shard_map.46 = bf16[384,1536]{1,0:T(8,128)(2,1)} custom-call(bf16[384,1536]{1,0:T(8,128)(2,1)} %tok_hbm.1, f32[1,1536]{1,0:T(1,128)} %reshape.3.gain_ref, bf16[3,1536,1536]{2,1,0:T(8,128)(2,1)} %bitcast.1, bf16[1536,1536]{1,0:T(8,128)(2,1)} %wo_hbm.1), custom_call_target="tpu_custom_call" | custom-call | tf_op jit(solution)/shard_map/pallas_call | solution.py:376
  109.1 2.4 %copy.6 = bf16[384,1536]{1,0:T(8,128)(2,1)} copy(bf16[384,1536]{1,0:T(8,128)(2,1)} %shard_map.46) | data formatting | bytes 2359296

commit v4 on v3

--- a/solution.py
+++ b/solution.py
@@ -69,9 +69,9 @@
 
 def sublayer_kernel(
     rows_n, cols_n, tok_hbm, gain_ref, w_hbm, wo_hbm, out_ref,
-    tok, wide_w, out_w, stat_col, stats, normed, arrived, summed, attended, late_w, early,
-    tok_sem, w_sem, wo_sem, late_sem, st_send, st_recv, rs_send, rs_recv, at_send, at_recv,
-    x_send, x_recv, lw_send, lw_recv, la_send, la_recv,
+    tok, wide_w, stat_col, stats, normed, arrived, summed, attended, late_w,
+    tok_sem, w_sem, late_sem, st_send, st_recv, rs_send, rs_recv, at_send, at_recv,
+    lw_send, lw_recv, fw_send, fw_recv, la_send, la_recv,
 ):
     z = lax.axis_index("row")
     col = lax.axis_index("col")
@@ -100,29 +100,34 @@
         weight_copy(0, c).start()
         weight_copy(1, c).start()
 
-    wo_copy = pltpu.make_async_copy(wo_hbm, out_w, wo_sem)
-    wo_copy.start()
-
-    def late_rows(d):
-        return wo_hbm.at[pl.ds(d * half + (pairs - 1) * WIDE, WIDE)]
-
-    def late_copy(d):
-        return pltpu.make_async_copy(late_rows(d), late_w.at[col, d], late_sem.at[d])
-
-    def late_share(d):
-        return pltpu.make_async_remote_copy(
-            src_ref=late_rows(d), dst_ref=late_w.at[col, d], send_sem=lw_send.at[d],
-            recv_sem=lw_recv.at[d], device_id=partner, device_id_type=MESH,
-        )
-
-    def late_arrival(d):
-        return pltpu.make_async_remote_copy(
-            src_ref=late_rows(d), dst_ref=late_w.at[1 - col, d], send_sem=lw_send.at[d],
-            recv_sem=lw_recv.at[d], device_id=partner, device_id_type=MESH,
-        )
-
-    for d in range(2):
-        late_copy(d).start()
+    dp = lax.axis_index("dp")
+    side = dp % 2
+    sibling = {"dp": dp + 1 - 2 * side}
+    split = WIDE // 2
+
+    def own_copy(d, p):
+        rows = pl.ds(d * half + p * WIDE, WIDE)
+        return pltpu.make_async_copy(wo_hbm.at[rows], late_w.at[col, d, p], late_sem.at[d, p])
+
+    def share_copy(d, p, owner):
+        first = pl.multiple_of(d * half + p * WIDE + side * split, split)
+        at = pl.ds(pl.multiple_of(side * split, split), split)
+        return pltpu.make_async_remote_copy(
+            src_ref=wo_hbm.at[pl.ds(first, split)], dst_ref=late_w.at[owner, d, p, at],
+            send_sem=lw_send.at[d, p], recv_sem=lw_recv.at[d, p], device_id=partner,
+            device_id_type=MESH,
+        )
+
+    def hand_copy(d, p, which):
+        piece = late_w.at[1 - col, d, p, pl.ds(pl.multiple_of(which * split, split), split)]
+        return pltpu.make_async_remote_copy(
+            src_ref=piece, dst_ref=piece, send_sem=fw_send.at[d, p],
+            recv_sem=fw_recv.at[d, p], device_id=sibling, device_id_type=MESH,
+        )
+
+    blocks = [(d, p) for p in range(pairs) for d in range(2)]
+    for d, p in blocks:
+        own_copy(d, p).start()
 
     barrier = pltpu.get_barrier_semaphore()
     for o in range(1, rows_n):
@@ -130,6 +135,7 @@
             barrier, inc=1, device_id={"row": lax.rem(z + o, rows_n)}, device_id_type=MESH
         )
     pl.semaphore_signal(barrier, inc=1, device_id=partner, device_id_type=MESH)
+    pl.semaphore_signal(barrier, inc=1, device_id=sibling, device_id_type=MESH)
 
     tok_copy.wait()
 
@@ -145,7 +151,7 @@
 
     stats[z, 0] = stat_col[0].T[0:8]
     stats[z, 1] = stat_col[1].T[0:8]
-    pl.semaphore_wait(barrier, rows_n)
+    pl.semaphore_wait(barrier, rows_n + 1)
 
     def stat_copy(o):
         return pltpu.make_async_remote_copy(
@@ -163,8 +169,8 @@
 
     for o in range(1, rows_n):
         stat_copy(o).start()
-    for d in range(2):
-        late_share(d).start()
+    for d, p in blocks:
+        share_copy(d, p, col).start()
     for o in range(1, rows_n):
         stat_arrival(o).wait_recv()
     mean = sum(stats[i, 0] for i in range(rows_n)) * (1.0 / rows_n)
@@ -207,17 +213,11 @@
             recv_sem=at_recv.at[d, p, i], device_id=back(d), device_id_type=MESH,
         )
 
-    def cross_copy(d, i, owner):
-        piece = attended.at[owner, d, pairs - 1, pl.ds(i * PIECE, PIECE)]
-        return pltpu.make_async_remote_copy(
-            src_ref=piece, dst_ref=piece, send_sem=la_send.at[d, i],
-            recv_sem=la_recv.at[d, i], device_id=partner, device_id_type=MESH,
-        )
-
-    def exchange(j, owner):
-        return pltpu.make_async_remote_copy(
-            src_ref=early.at[owner, j], dst_ref=early.at[owner, j], send_sem=x_send.at[j],
-            recv_sem=x_recv.at[j], device_id=partner, device_id_type=MESH,
+    def cross_copy(d, p, i, owner):
+        piece = attended.at[owner, d, p, pl.ds(i * PIECE, PIECE)]
+        return pltpu.make_async_remote_copy(
+            src_ref=piece, dst_ref=piece, send_sem=la_send.at[d, p, i],
+            recv_sem=la_recv.at[d, p, i], device_id=partner, device_id_type=MESH,
         )
 
     def attend_piece(d, p, i):
@@ -236,24 +236,9 @@
                 weights.astype(jnp.bfloat16), v, preferred_element_type=jnp.float32
             ).astype(jnp.bfloat16)
 
-    def project_early():
-        @pl.loop(0, tiles)
-        def _(j):
-            at = pl.ds(pl.multiple_of(j * WIDE, WIDE), WIDE)
-            total = jnp.zeros((tokens_n, WIDE), jnp.float32)
-            for d in range(2):
-                for p in range(pairs - 1):
-                    first = d * half + p * WIDE
-                    total = total + jnp.dot(
-                        attended[col, d, p], out_w[first:first + WIDE, at],
-                        preferred_element_type=jnp.float32,
-                    )
-            early[col, j] = total.astype(jnp.bfloat16)
-            exchange(j, col).start()
-
     last_place = rows_n - 1
     slots = chunks + 2 * SKEW * last_place
-    early_slot = chunks - 4 + SKEW * (last_place + jnp.maximum(z, last_place - z))
+    hand_slots = [min(4 + 2 * b, slots - 1) for b in range(len(blocks))]
 
     @pl.loop(0, slots)
     def _(t):
@@ -305,30 +290,28 @@
                     def _():
                         attended_copy(d, p, i).start()
 
-                    @pl.when(p == pairs - 1)
-                    def _():
-                        cross_copy(d, i, col).start()
-
-        @pl.when(t == early_slot)
-        def _():
-            wo_copy.wait()
-            project_early()
-
-    for d in range(2):
-        late_copy(d).wait()
-        late_arrival(d).wait_recv()
+                    cross_copy(d, p, i, col).start()
+
+        for (d, p), slot in zip(blocks, hand_slots):
+            @pl.when(t == slot)
+            def _():
+                share_copy(d, p, 1 - col).wait_recv()
+                hand_copy(d, p, side).start()
+
+    for d, p in blocks:
+        own_copy(d, p).wait()
+        hand_copy(d, p, 1 - side).wait_recv()
         for i in range(pieces):
-            cross_copy(d, i, 1 - col).wait_recv()
+            cross_copy(d, p, i, 1 - col).wait_recv()
 
     @pl.loop(0, tiles)
     def _(j):
         at = pl.ds(pl.multiple_of(j * WIDE, WIDE), WIDE)
-        exchange(j, 1 - col).wait_recv()
-        total = early[0, j].astype(jnp.float32) + early[1, j].astype(jnp.float32)
+        total = jnp.zeros((tokens_n, WIDE), jnp.float32)
         for owner in range(2):
-            for d in range(2):
+            for d, p in blocks:
                 total = total + jnp.dot(
-                    attended[owner, d, pairs - 1], late_w[owner, d, :, at],
+                    attended[owner, d, p], late_w[owner, d, p, :, at],
                     preferred_element_type=jnp.float32,
                 )
         out_ref[:, at] = total.astype(jnp.bfloat16)
@@ -352,14 +335,11 @@
                 for i in range(pieces):
                     attended_copy(d, p, i).wait_send()
 
-    @pl.loop(0, tiles)
-    def _(j):
-        exchange(j, col).wait_send()
-
-    for d in range(2):
-        late_share(d).wait_send()
+    for d, p in blocks:
+        share_copy(d, p, col).wait_send()
+        hand_copy(d, p, side).wait_send()
         for i in range(pieces):
-            cross_copy(d, i, col).wait_send()
+            cross_copy(d, p, i, col).wait_send()
 
 
 def fused_shards(rows_n, cols_n, tokens, norm_gain, qkv_weight, out_weight):
@@ -367,7 +347,6 @@
     head_columns = qkv_weight.shape[2]
     pairs = head_columns // (2 * WIDE)
     chunks = 3 * pairs
-    tiles = block // WIDE
     pieces = tokens_n // PIECE
     any_space = pl.BlockSpec(memory_space=pl.ANY)
     vmem = pl.BlockSpec(memory_space=pltpu.VMEM)
@@ -381,21 +360,19 @@
         scratch_shapes=[
             pltpu.VMEM((tokens_n, block), bf16),
             pltpu.VMEM((2, chunks, block, WIDE), bf16),
-            pltpu.VMEM((head_columns, block), bf16),
             pltpu.VMEM((2, tokens_n, 128), f32),
             pltpu.VMEM((rows_n, 2, 8, tokens_n), f32),
             pltpu.VMEM((tokens_n, block), bf16),
             pltpu.VMEM((2, chunks, tokens_n, WIDE), bf16),
             pltpu.VMEM((2, chunks, tokens_n, WIDE), bf16),
             pltpu.VMEM((2, 2, pairs, tokens_n, WIDE), bf16),
-            pltpu.VMEM((2, 2, WIDE, block), bf16),
-            pltpu.VMEM((2, tiles, tokens_n, WIDE), bf16),
-            dma, dma((2, chunks)), dma, dma((2,)),
+            pltpu.VMEM((2, 2, pairs, WIDE, block), bf16),
+            dma, dma((2, chunks)), dma((2, pairs)),
             dma((rows_n,)), dma((rows_n,)),
             dma((2, chunks, PARTS)), dma((2, chunks, PARTS)),
             dma((2, pairs, pieces)), dma((2, pairs, pieces)),
-            dma((tiles,)), dma((tiles,)), dma((2,)), dma((2,)),
-            dma((2, pieces)), dma((2, pieces)),
+            dma((2, pairs)), dma((2, pairs)), dma((2, pairs)), dma((2, pairs)),
+            dma((2, pairs, pieces)), dma((2, pairs, pieces)),
         ],
         compiler_params=pltpu.CompilerParams(
             collective_id=0, has_side_effects=True, vmem_limit_bytes=60 * 1024 * 1024
@@ -411,7 +388,7 @@
     def body(tokens, norm_gain, qkv_weight, out_weight):
         tokens_n, block = tokens.shape
         fits = (
-            cols_n == 2 and rows_n >= 2 and qkv_weight.shape[2] % (2 * WIDE) == 0
+            cols_n == 2 and mesh.shape["dp"] % 2 == 0 and rows_n >= 2 and qkv_weight.shape[2] % (2 * WIDE) == 0
             and qkv_weight.shape[2] >= 4 * WIDE
             and block % WIDE == 0 and tokens_n % 128 == 0
         )

time: 112 us -> 102 us (0.911)
  Pallas kernels: 108 us -> 97.8 us
    pallas_call x1, Pallas kernels: 108 us -> 97.8 us  [fused_shards(): pl.pallas_call(functools.partial(sublayer_kernel, rows_n, cols_n), out_sh...]
where the time goes in v4:
time: 102 us; the launch traced here: 101 us
  Pallas kernels  97.8 us (96%)
  local copies, waits for them, and re-layouts  3.65 us (4%)
    pallas_call x1, Pallas kernels, fused_shards(): pl.pallas_call(functools.partial(sublayer_kernel, rows_n, cols_n), out_sh...  97.8 us
    unnamed x1, local copies, waits for them, and re-layouts  2.36 us

profile of v4, /device:TPU:0, one launch (start us, length us, event | category | flops | bytes accessed | tf_op | source)
XLA Modules:
  0.0 101.5 jit_solution(9908469070567574225)
XLA Ops:
  0.0 1.3 %reshape.3.gain_ref = f32[1,1536]{1,0:T(1,128)} reshape(f32[1536]{0:T(1024)} %param.5) | data formatting | bytes 12288 | tf_op jit(solution)/shard_map/reshape | solution.py:380
  1.3 97.8 %shard_map.46 = bf16[384,1536]{1,0:T(8,128)(2,1)} custom-call(bf16[384,1536]{1,0:T(8,128)(2,1)} %tok_hbm.1, f32[1,1536]{1,0:T(1,128)} %reshape.3.gain_ref, bf16[3,1536,1536]{2,1,0:T(8,128)(2,1)} %bitcast.1, bf16[1536,1536]{1,0:T(8,128)(2,1)} %wo_hbm.1), custom_call_target="tpu_custom_call" | custom-call | tf_op jit(solution)/shard_map/pallas_call | solution.py:355
  99.1 2.4 %copy.6 = bf16[384,1536]{1,0:T(8,128)(2,1)} copy(bf16[384,1536]{1,0:T(8,128)(2,1)} %shard_map.46) | data formatting | bytes 2359296
